TPU v7x, 32 devices: a whole 2x2x4 slice. The times are simulated.
32 devices in a mesh: scen: 8 (over z, x), blk: 4 (over y, core).
Axes of the slice: x: 2, y: 2, z: 4, core: 2. Of those that a mesh axis runs over, the one named last changes fastest.
Arguments:
- cons_matrix: bfloat16 [2048, 4096], P(None, 'blk'), may hold values from -0.09375 to 0.09375
- row_scale: float32 [512, 2048], P('scen'), may hold values from 0.5 to 2
- rhs: float32 [512, 2048], P('scen'), may hold values from -6 to 6
- cons_mult: float32 [512, 2048], P('scen'), may hold values from -3 to 3
- cost: float32 [512, 4096], P('scen', 'blk'), may hold values from -6 to 6
- ph_mult: float32 [512, 4096], P('scen', 'blk'), may hold values from -3 to 3
- start: float32 [512, 4096], P('scen', 'blk'), may hold values from -3 to 3
- consensus: float32 [4096], P('blk'), may hold values from -3 to 3
- upper: float32 [4096], P('blk'), may hold values from 0.3 to 1.5
- prob: float32 [512], P('scen'), may hold values from 1 to 30, as said below
Outputs:
- solutions: float32 [512, 4096], P('scen', 'blk')
- mult_new: float32 [512, 2048], P('scen', 'blk')
- z_new: float32 [4096], P('blk')
- w_new: float32 [512, 4096], P('scen', 'blk')
- primal_res: float32 [], replicated
- dual_res: float32 [], replicated
Inputs may be any that keep to these rules, and one draw needn't show every extreme that they name: prob is positive.
All inputs are finite; a program needn't handle non-finite values.
Results may differ from a plain program's by a relative error of at most 0.0017.
Values may be sent and summed in bfloat16 or wider, within the bound.
A program may use at most 64 MiB of HBM per device.

v0:
```python
import jax
import jax.numpy as jnp
from jax import lax
from jax.sharding import PartitionSpec as P

NV = 4096
ITERS = 8
penalty = 1.0
aug_weight = 1.0
step_size = 0.05
eps = 1e-06


def per_device(
    cons_matrix, row_scale, rhs, cons_mult, cost, ph_mult, start, consensus, upper, prob
):
    n_blk = lax.axis_size("blk")
    n_scen = lax.axis_size("scen")
    share_rows = cons_matrix.shape[0] // n_blk
    first_row = lax.axis_index("blk") * share_rows
    own_scale = lax.dynamic_slice_in_dim(row_scale, first_row, share_rows, 1)
    own_rhs = lax.dynamic_slice_in_dim(rhs, first_row, share_rows, 1)
    own_mult = lax.dynamic_slice_in_dim(cons_mult, first_row, share_rows, 1)
    contract = (((1,), (1,)), ((), ()))
    x_now = start
    low_box = -upper[None, :]
    high_box = upper[None, :]
    for step in range(ITERS):
        partial_value = lax.dot_general(
            x_now.astype(jnp.bfloat16), cons_matrix, contract, preferred_element_type=jnp.float32
        )
        prod_share = lax.psum_scatter(partial_value, "blk", scatter_dimension=1, tiled=True)
        weighted_share = (
            own_scale * (own_mult + aug_weight * (own_scale * prod_share - own_rhs))
        ).astype(jnp.bfloat16)
        back = jnp.dot(
            lax.all_gather(weighted_share, "blk", axis=1, tiled=True),
            cons_matrix,
            preferred_element_type=jnp.float32,
        )
        grad = cost + ph_mult + penalty * (x_now - consensus[None, :]) + back
        x_now = jnp.clip(x_now - step_size * grad, low_box, high_box)
    partial_end = lax.dot_general(
        x_now.astype(jnp.bfloat16), cons_matrix, contract, preferred_element_type=jnp.float32
    )
    prod_end = lax.psum_scatter(partial_end, "blk", scatter_dimension=1, tiled=True)
    mult_new = own_mult + aug_weight * (own_scale * prod_end - own_rhs)
    weighted_x = prob[:, None] * x_now
    local_sum = jnp.sum(weighted_x, axis=0)
    local_total = jnp.sum(prob)
    sums, total = lax.psum((local_sum, local_total), "scen")
    z_new = sums / total
    primal_local = jnp.sum(prob[:, None] * (x_now - z_new[None, :]) ** 2)
    dual_local = jnp.sum((z_new - consensus) ** 2) * (1.0 / n_scen)
    primal_sum, dual_sum = lax.psum((primal_local, dual_local), ("scen", "blk"))
    w_new = ph_mult + penalty * (x_now - z_new[None, :])
    primal_res = jnp.sqrt(primal_sum / (total * NV) + eps)
    dual_res = penalty * jnp.sqrt(dual_sum / NV + eps)
    return (x_now, mult_new, z_new, w_new, primal_res, dual_res)


def solution(mesh):
    in_specs = (
        P(None, "blk"),
        P("scen", None),
        P("scen", None),
        P("scen", None),
        P("scen", "blk"),
        P("scen", "blk"),
        P("scen", "blk"),
        P("blk"),
        P("blk"),
        P("scen"),
    )
    out_specs = (P("scen", "blk"), P("scen", "blk"), P("blk"), P("scen", "blk"), P(), P())
    return jax.shard_map(
        per_device, mesh=mesh, in_specs=in_specs, out_specs=out_specs, check_vma=False
    )
```

profile of v0, /device:TPU:12, one launch (start us, length us, event | category | flops | bytes accessed | tf_op | source)
XLA Modules:
  0.0 364.3 jit_solution(18422176172987149110)
XLA Ops:
  7.3 4.6 %fusion.48 = f32[64,2048]{1,0:T(8,128)} fusion(bf16[2048,1024]{1,0:T(8,128)(2,1)} %param.10, f32[64,1024]{1,0:T(8,128)} %param.16), kind=kOutput, calls=%fused_computation.68 | convolution fusion | flops 268500992 | bytes 4980736 | tf_op jit(solution)/shard_map/dot_general | solution.py:29
  12.1 21.8 %reduce-scatter.10.cloned.1.call-done = f32[64,512]{1,0:T(8,128)} async-done(((f32[64,2048]{1,0:T(8,128)}), f32[64,512]{1,0:T(8,128)}) %reduce-scatter.10.cloned.1.call-update) | async-done | bytes 131088 | tf_op jit(solution)/shard_map/reduce_scatter | solution.py:32
  35.0 5.9 %all_gather.24 = bf16[64,2048]{1,0:T(8,128)(2,1)S(1)} all-gather(bf16[64,512]{1,0:T(8,128)(2,1)S(1)} %multiply_convert_fusion.7), channel_id=1, replica_groups=mesh['scen'=8,'blk'=4] {'blk'}, dimensions={1}, use_global_device_ids=true | all-gather | bytes 327680 | tf_op jit(solution)/shard_map/all_gather | solution.py:37
  40.9 3.1 fusion.17
  46.3 21.8 %reduce-scatter.12.cloned.1.call-done = f32[64,512]{1,0:T(8,128)} async-done(((f32[64,2048]{1,0:T(8,128)}), f32[64,512]{1,0:T(8,128)}) %reduce-scatter.12.cloned.1.call-update) | async-done | bytes 131088 | tf_op jit(solution)/shard_map/reduce_scatter | solution.py:32
  69.2 5.9 %all_gather.25 = bf16[64,2048]{1,0:T(8,128)(2,1)S(1)} all-gather(bf16[64,512]{1,0:T(8,128)(2,1)S(1)} %multiply_convert_fusion.6), channel_id=1, replica_groups=mesh['scen'=8,'blk'=4] {'blk'}, dimensions={1}, use_global_device_ids=true | all-gather | bytes 327680 | tf_op jit(solution)/shard_map/all_gather | solution.py:37
  75.1 3.1 fusion.19
  80.5 21.8 %reduce-scatter.14.cloned.1.call-done = f32[64,512]{1,0:T(8,128)} async-done(((f32[64,2048]{1,0:T(8,128)}), f32[64,512]{1,0:T(8,128)}) %reduce-scatter.14.cloned.1.call-update) | async-done | bytes 131088 | tf_op jit(solution)/shard_map/reduce_scatter | solution.py:32
  103.3 5.9 %all_gather.26 = bf16[64,2048]{1,0:T(8,128)(2,1)S(1)} all-gather(bf16[64,512]{1,0:T(8,128)(2,1)S(1)} %multiply_convert_fusion.5), channel_id=1, replica_groups=mesh['scen'=8,'blk'=4] {'blk'}, dimensions={1}, use_global_device_ids=true | all-gather | bytes 327680 | tf_op jit(solution)/shard_map/all_gather | solution.py:37
  114.6 21.8 %reduce-scatter.16.cloned.1.call-done = f32[64,512]{1,0:T(8,128)} async-done(((f32[64,2048]{1,0:T(8,128)}), f32[64,512]{1,0:T(8,128)}) %reduce-scatter.16.cloned.1.call-update) | async-done | bytes 131088 | tf_op jit(solution)/shard_map/reduce_scatter | solution.py:32
  137.5 5.9 %all_gather.27 = bf16[64,2048]{1,0:T(8,128)(2,1)S(1)} all-gather(bf16[64,512]{1,0:T(8,128)(2,1)S(1)} %multiply_convert_fusion.4), channel_id=1, replica_groups=mesh['scen'=8,'blk'=4] {'blk'}, dimensions={1}, use_global_device_ids=true | all-gather | bytes 327680 | tf_op jit(solution)/shard_map/all_gather | solution.py:37
  143.4 3.1 fusion.23
  148.8 21.8 %reduce-scatter.18.cloned.1.call-done = f32[64,512]{1,0:T(8,128)} async-done(((f32[64,2048]{1,0:T(8,128)}), f32[64,512]{1,0:T(8,128)}) %reduce-scatter.18.cloned.1.call-update) | async-done | bytes 131088 | tf_op jit(solution)/shard_map/reduce_scatter | solution.py:32
  171.6 5.9 %all_gather.28 = bf16[64,2048]{1,0:T(8,128)(2,1)S(1)} all-gather(bf16[64,512]{1,0:T(8,128)(2,1)S(1)} %multiply_convert_fusion.3), channel_id=1, replica_groups=mesh['scen'=8,'blk'=4] {'blk'}, dimensions={1}, use_global_device_ids=true | all-gather | bytes 327680 | tf_op jit(solution)/shard_map/all_gather | solution.py:37
  183.1 21.6 %reduce-scatter.20.cloned.1.call-done = f32[64,512]{1,0:T(8,128)} async-done(((f32[64,2048]{1,0:T(8,128)}), f32[64,512]{1,0:T(8,128)}) %reduce-scatter.20.cloned.1.call-update) | async-done | bytes 131088 | tf_op jit(solution)/shard_map/reduce_scatter | solution.py:32
  205.8 5.9 %all_gather.29 = bf16[64,2048]{1,0:T(8,128)(2,1)S(1)} all-gather(bf16[64,512]{1,0:T(8,128)(2,1)S(1)} %multiply_convert_fusion.2), channel_id=1, replica_groups=mesh['scen'=8,'blk'=4] {'blk'}, dimensions={1}, use_global_device_ids=true | all-gather | bytes 327680 | tf_op jit(solution)/shard_map/all_gather | solution.py:37
  211.7 3.1 fusion.27
  217.1 21.8 %reduce-scatter.22.cloned.1.call-done = f32[64,512]{1,0:T(8,128)} async-done(((f32[64,2048]{1,0:T(8,128)}), f32[64,512]{1,0:T(8,128)}) %reduce-scatter.22.cloned.1.call-update) | async-done | bytes 131088 | tf_op jit(solution)/shard_map/reduce_scatter | solution.py:32
  240.0 5.9 %all_gather.30 = bf16[64,2048]{1,0:T(8,128)(2,1)S(1)} all-gather(bf16[64,512]{1,0:T(8,128)(2,1)S(1)} %multiply_convert_fusion.1), channel_id=1, replica_groups=mesh['scen'=8,'blk'=4] {'blk'}, dimensions={1}, use_global_device_ids=true | all-gather | bytes 327680 | tf_op jit(solution)/shard_map/all_gather | solution.py:37
  251.3 21.8 %reduce-scatter.24.cloned.1.call-done = f32[64,512]{1,0:T(8,128)} async-done(((f32[64,2048]{1,0:T(8,128)}), f32[64,512]{1,0:T(8,128)}) %reduce-scatter.24.cloned.1.call-update) | async-done | bytes 131088 | tf_op jit(solution)/shard_map/reduce_scatter | solution.py:32
  274.1 5.9 %all_gather.31 = bf16[64,2048]{1,0:T(8,128)(2,1)S(1)} all-gather(bf16[64,512]{1,0:T(8,128)(2,1)S(1)} %multiply_convert_fusion), channel_id=1, replica_groups=mesh['scen'=8,'blk'=4] {'blk'}, dimensions={1}, use_global_device_ids=true | all-gather | bytes 327680 | tf_op jit(solution)/shard_map/all_gather | solution.py:37
  280.0 3.1 multiply_reduce_fusion.1
  286.0 19.5 %all-reduce.1 = (f32[1024]{0:T(1024)S(1)}, f32[]{:T(128)}) all-reduce(f32[1024]{0:T(1024)S(1)} %get-tuple-element.14, f32[]{:T(128)} %reduce_sum.37), channel_id=1, replica_groups=mesh['scen'=8,'blk'=4] {'scen'}, use_global_device_ids=true, to_apply=%region_10.11 | all-reduce | flops 1025 | bytes 8200 | tf_op jit(solution)/shard_map/psum | solution.py:51
  308.7 43.1 %all-reduce = (f32[]{:T(128)}, f32[]{:T(128)}) all-reduce(f32[]{:T(128)} %get-tuple-element.12, f32[]{:T(128)S(6)} %mul.128), channel_id=1, replica_groups=mesh['scen'=8,'blk'=4] {'scen','blk'}, use_global_device_ids=true, to_apply=%region_14.15 | all-reduce | flops 2 | bytes 16 | tf_op jit(solution)/shard_map/psum | solution.py:55
  (82 shorter events, 41.2 us)
Async XLA Ops:
  7.2 33.8 %copy-start.12 = (f32[64,1024]{1,0:T(8,128)S(1)}, f32[64,1024]{1,0:T(8,128)}, u32[]{:S(2)}) copy-start(f32[64,1024]{1,0:T(8,128)} %param.16) | copy-start | bytes 786436
  7.2 26.7 %copy-start.8 = (f32[64,2048]{1,0:T(8,128)S(1)}, f32[64,2048]{1,0:T(8,128)}, u32[]{:S(2)}) copy-start(f32[64,2048]{1,0:T(8,128)} %param.12) | copy-start | bytes 1572868
  7.2 26.7 %copy-start.9 = (f32[64,2048]{1,0:T(8,128)S(1)}, f32[64,2048]{1,0:T(8,128)}, u32[]{:S(2)}) copy-start(f32[64,2048]{1,0:T(8,128)} %param.13) | copy-start | bytes 1572868
  7.2 26.7 %copy-start.10 = (f32[64,2048]{1,0:T(8,128)S(1)}, f32[64,2048]{1,0:T(8,128)}, u32[]{:S(2)}) copy-start(f32[64,2048]{1,0:T(8,128)} %param.11) | copy-start | bytes 1572868
  7.2 33.7 %copy-start.15 = (f32[1024]{0:T(1024)S(1)}, f32[1024]{0:T(1024)}, u32[]{:S(2)}) copy-start(f32[1024]{0:T(1024)} %param.17) | copy-start | bytes 12292
  7.2 26.6 %reduce-scatter.10.cloned.1.call-start = ((), (), s32[]{:S(2)}) async-start(), calls=%async_computation.9 | async-start | bytes 655360 | tf_op jit(solution)/shard_map/reduce_scatter | solution.py:32
  11.9 56.2 %reduce-scatter.12.cloned.1.call-start = ((), (), s32[]{:S(2)}) async-start(), calls=%async_computation.10 | async-start | bytes 655360 | tf_op jit(solution)/shard_map/reduce_scatter | solution.py:32
  33.9 10.1 %copy-start = (bf16[2048,1024]{1,0:T(8,128)(2,1)S(1)}, bf16[2048,1024]{1,0:T(8,128)(2,1)}, u32[]{:S(2)}) copy-start(bf16[2048,1024]{1,0:T(8,128)(2,1)} %param.10) | copy-start | bytes 12582916
  46.3 56.0 %reduce-scatter.14.cloned.1.call-start = ((), (), s32[]{:S(2)}) async-start(), calls=%async_computation.11 | async-start | bytes 655360 | tf_op jit(solution)/shard_map/reduce_scatter | solution.py:32
  68.1 10.1 %copy-start.1 = (bf16[2048,1024]{1,0:T(8,128)(2,1)S(1)}, bf16[2048,1024]{1,0:T(8,128)(2,1)}, u32[]{:S(2)}) copy-start(bf16[2048,1024]{1,0:T(8,128)(2,1)} %param.10) | copy-start | bytes 12582916
  80.4 56.0 %reduce-scatter.16.cloned.1.call-start = ((), (), s32[]{:S(2)}) async-start(), calls=%async_computation.12 | async-start | bytes 655360 | tf_op jit(solution)/shard_map/reduce_scatter | solution.py:32
  102.2 10.1 %copy-start.2 = (bf16[2048,1024]{1,0:T(8,128)(2,1)S(1)}, bf16[2048,1024]{1,0:T(8,128)(2,1)}, u32[]{:S(2)}) copy-start(bf16[2048,1024]{1,0:T(8,128)(2,1)} %param.10) | copy-start | bytes 12582916
  114.6 56.0 %reduce-scatter.18.cloned.1.call-start = ((), (), s32[]{:S(2)}) async-start(), calls=%async_computation.13 | async-start | bytes 655360 | tf_op jit(solution)/shard_map/reduce_scatter | solution.py:32
  136.4 10.1 %copy-start.3 = (bf16[2048,1024]{1,0:T(8,128)(2,1)S(1)}, bf16[2048,1024]{1,0:T(8,128)(2,1)}, u32[]{:S(2)}) copy-start(bf16[2048,1024]{1,0:T(8,128)(2,1)} %param.10) | copy-start | bytes 12582916
  148.7 56.0 %reduce-scatter.20.cloned.1.call-start = ((), (), s32[]{:S(2)}) async-start(), calls=%async_computation.14 | async-start | bytes 655360 | tf_op jit(solution)/shard_map/reduce_scatter | solution.py:32
  182.9 56.0 %reduce-scatter.22.cloned.1.call-start = ((), (), s32[]{:S(2)}) async-start(), calls=%async_computation.15 | async-start | bytes 655360 | tf_op jit(solution)/shard_map/reduce_scatter | solution.py:32
  204.7 10.1 %copy-start.5 = (bf16[2048,1024]{1,0:T(8,128)(2,1)S(1)}, bf16[2048,1024]{1,0:T(8,128)(2,1)}, u32[]{:S(2)}) copy-start(bf16[2048,1024]{1,0:T(8,128)(2,1)} %param.10) | copy-start | bytes 12582916
  217.1 56.0 %reduce-scatter.24.cloned.1.call-start = ((), (), s32[]{:S(2)}) async-start(), calls=%async_computation.16 | async-start | bytes 655360 | tf_op jit(solution)/shard_map/reduce_scatter | solution.py:32
  238.9 10.1 %copy-start.6 = (bf16[2048,1024]{1,0:T(8,128)(2,1)S(1)}, bf16[2048,1024]{1,0:T(8,128)(2,1)}, u32[]{:S(2)}) copy-start(bf16[2048,1024]{1,0:T(8,128)(2,1)} %param.10) | copy-start | bytes 12582916
  249.0 31.1 %copy-start.18 = (f32[64]{0:T(128)S(1)}, f32[64]{0:T(128)}, u32[]{:S(2)}) copy-start(f32[64]{0:T(128)} %param.19) | copy-start | bytes 772
  251.2 102.7 %reduce-scatter.26.cloned.1.call-start = ((), (), s32[]{:S(2)}) async-start(), calls=%async_computation.17 | async-start | bytes 655360 | tf_op jit(solution)/shard_map/reduce_scatter | solution.py:46
  273.0 10.2 %copy-start.7 = (bf16[2048,1024]{1,0:T(8,128)(2,1)S(1)}, bf16[2048,1024]{1,0:T(8,128)(2,1)}, u32[]{:S(2)}) copy-start(bf16[2048,1024]{1,0:T(8,128)(2,1)} %param.10) | copy-start | bytes 12582916
  283.2 72.3 %copy-start.11 = (f32[64,1024]{1,0:T(8,128)}, f32[64,1024]{1,0:T(8,128)S(1)}, u32[]{:S(2)}) copy-start(f32[64,1024]{1,0:T(8,128)S(1)} %get-tuple-element.15) | copy-start | bytes 786436
  306.7 48.7 %copy-start.17 = (f32[1024]{0:T(1024)}, f32[1024]{0:T(1024)S(1)}, u32[]{:S(2)}) copy-start(f32[1024]{0:T(1024)S(1)} %get-tuple-element.11) | copy-start | bytes 12292
  (4 other events, 24.5 us)
Sparse Core Ops, SparseCore 0:
  12.0 21.8 reduce-scatter.9
  46.4 21.6 reduce-scatter.11
  80.5 21.6 reduce-scatter.13
  114.7 21.6 reduce-scatter.15
  148.9 21.6 reduce-scatter.17
  183.0 21.6 reduce-scatter.19
  217.2 21.6 reduce-scatter.21
  251.3 21.6 reduce-scatter.23
  285.5 21.6 reduce-scatter.25
where the time goes:
time: 365 us; the launch traced here: 364 us
  waiting for transfers between devices  174 us (48%)
  blocking collectives  110 us (30%)
  matrix products  46.9 us (13%)
  between operations  19.1 us (5%)
  other arithmetic  13.6 us (4%)
    reduce_scatter x8, waiting for transfers between devices, per_device(): lax.psum_scatter(partial_value, 'blk', scatter_dimension=1, tiled=True)  174 us
    all_gather x8, blocking collectives, per_device(): lax.all_gather(weighted_share, 'blk', axis=1, tiled=True)  47.3 us
    psum x1, blocking collectives, per_device(): primal_sum, dual_sum = lax.psum((primal_local, dual_local), ('scen', 'blk'))  43.1 us
    dot_general x8, matrix products, per_device(): jnp.dot(lax.all_gather(weighted_share, 'blk', axis=1, tiled=True), cons_m...  24.7 us
    dot_general x9, matrix products, per_device(): lax.dot_general(x_now.astype(jnp.bfloat16), cons_matrix, contract, prefer...  22.2 us
    psum x1, blocking collectives, per_device(): sums, total = lax.psum((local_sum, local_total), 'scen')  19.5 us
    convert_element_type x8, other arithmetic, per_device(): weighted_share = (own_scale * (own_mult + aug_weight * (own_scale * prod_...  8.73 us
  transfers between devices with their start and end apart: 9, of which 8 were waited for; matrix products, arithmetic and copies ran while one was open for 1% of the time, Pallas kernels for 0%

commit v1 on v0

--- a/solution.py
+++ b/solution.py
@@ -52,7 +52,7 @@
     z_new = sums / total
     primal_local = jnp.sum(prob[:, None] * (x_now - z_new[None, :]) ** 2)
     dual_local = jnp.sum((z_new - consensus) ** 2) * (1.0 / n_scen)
-    primal_sum, dual_sum = lax.psum((primal_local, dual_local), ("scen", "blk"))
+    primal_sum, dual_sum = lax.psum(lax.psum((primal_local, dual_local), "blk"), "scen")
     w_new = ph_mult + penalty * (x_now - z_new[None, :])
     primal_res = jnp.sqrt(primal_sum / (total * NV) + eps)
     dual_res = penalty * jnp.sqrt(dual_sum / NV + eps)

time: 365 us -> 351 us (0.962); the launches traced: 364 us -> 345 us
  blocking collectives: 110 us -> 90.8 us
    psum x1 -> x2, blocking collectives: 43.1 us -> 24 us  [the longest x1 17.7 us: per_device(): lax.psum(lax.psum((primal_local, dual_local), 'blk'), 'scen')]
where the time goes in v1:
time: 351 us; the launch traced here: 345 us
  waiting for transfers between devices  174 us (50%)
  blocking collectives  90.8 us (26%)
  matrix products  46.9 us (13%)
  between operations  19.1 us (5%)
  other arithmetic  13.6 us (4%)
    reduce_scatter x8, waiting for transfers between devices, per_device(): lax.psum_scatter(partial_value, 'blk', scatter_dimension=1, tiled=True)  174 us
    all_gather x8, blocking collectives, per_device(): lax.all_gather(weighted_share, 'blk', axis=1, tiled=True)  47.3 us
    dot_general x8, matrix products, per_device(): jnp.dot(lax.all_gather(weighted_share, 'blk', axis=1, tiled=True), cons_m...  24.7 us
    dot_general x9, matrix products, per_device(): lax.dot_general(x_now.astype(jnp.bfloat16), cons_matrix, contract, prefer...  22.2 us
    psum x1, blocking collectives, per_device(): sums, total = lax.psum((local_sum, local_total), 'scen')  19.5 us
    psum x1, blocking collectives, per_device(): lax.psum(lax.psum((primal_local, dual_local), 'blk'), 'scen')  17.7 us
    convert_element_type x8, other arithmetic, per_device(): weighted_share = (own_scale * (own_mult + aug_weight * (own_scale * prod_...  8.73 us
  transfers between devices with their start and end apart: 9, of which 8 were waited for; matrix products, arithmetic and copies ran while one was open for 1% of the time, Pallas kernels for 0%

profile of v1, /device:TPU:12, one launch (start us, length us, event | category | flops | bytes accessed | tf_op | source)
XLA Modules:
  0.0 345.2 jit_solution(7482902403306042536)
XLA Ops:
  7.3 4.6 %fusion.48 = f32[64,2048]{1,0:T(8,128)} fusion(bf16[2048,1024]{1,0:T(8,128)(2,1)} %param.10, f32[64,1024]{1,0:T(8,128)} %param.16), kind=kOutput, calls=%fused_computation.68 | convolution fusion | flops 268500992 | bytes 4980736 | tf_op jit(solution)/shard_map/dot_general | solution.py:29
  12.1 21.8 %reduce-scatter.10.cloned.1.call-done = f32[64,512]{1,0:T(8,128)} async-done(((f32[64,2048]{1,0:T(8,128)}), f32[64,512]{1,0:T(8,128)}) %reduce-scatter.10.cloned.1.call-update) | async-done | bytes 131088 | tf_op jit(solution)/shard_map/reduce_scatter | solution.py:32
  35.0 5.9 %all_gather.24 = bf16[64,2048]{1,0:T(8,128)(2,1)S(1)} all-gather(bf16[64,512]{1,0:T(8,128)(2,1)S(1)} %multiply_convert_fusion.7), channel_id=1, replica_groups=mesh['scen'=8,'blk'=4] {'blk'}, dimensions={1}, use_global_device_ids=true | all-gather | bytes 327680 | tf_op jit(solution)/shard_map/all_gather | solution.py:37
  40.9 3.1 fusion.17
  46.3 21.8 %reduce-scatter.12.cloned.1.call-done = f32[64,512]{1,0:T(8,128)} async-done(((f32[64,2048]{1,0:T(8,128)}), f32[64,512]{1,0:T(8,128)}) %reduce-scatter.12.cloned.1.call-update) | async-done | bytes 131088 | tf_op jit(solution)/shard_map/reduce_scatter | solution.py:32
  69.2 5.9 %all_gather.25 = bf16[64,2048]{1,0:T(8,128)(2,1)S(1)} all-gather(bf16[64,512]{1,0:T(8,128)(2,1)S(1)} %multiply_convert_fusion.6), channel_id=1, replica_groups=mesh['scen'=8,'blk'=4] {'blk'}, dimensions={1}, use_global_device_ids=true | all-gather | bytes 327680 | tf_op jit(solution)/shard_map/all_gather | solution.py:37
  75.1 3.1 fusion.19
  80.5 21.8 %reduce-scatter.14.cloned.1.call-done = f32[64,512]{1,0:T(8,128)} async-done(((f32[64,2048]{1,0:T(8,128)}), f32[64,512]{1,0:T(8,128)}) %reduce-scatter.14.cloned.1.call-update) | async-done | bytes 131088 | tf_op jit(solution)/shard_map/reduce_scatter | solution.py:32
  103.3 5.9 %all_gather.26 = bf16[64,2048]{1,0:T(8,128)(2,1)S(1)} all-gather(bf16[64,512]{1,0:T(8,128)(2,1)S(1)} %multiply_convert_fusion.5), channel_id=1, replica_groups=mesh['scen'=8,'blk'=4] {'blk'}, dimensions={1}, use_global_device_ids=true | all-gather | bytes 327680 | tf_op jit(solution)/shard_map/all_gather | solution.py:37
  109.2 3.1 fusion.21
  114.6 21.8 %reduce-scatter.16.cloned.1.call-done = f32[64,512]{1,0:T(8,128)} async-done(((f32[64,2048]{1,0:T(8,128)}), f32[64,512]{1,0:T(8,128)}) %reduce-scatter.16.cloned.1.call-update) | async-done | bytes 131088 | tf_op jit(solution)/shard_map/reduce_scatter | solution.py:32
  137.5 5.9 %all_gather.27 = bf16[64,2048]{1,0:T(8,128)(2,1)S(1)} all-gather(bf16[64,512]{1,0:T(8,128)(2,1)S(1)} %multiply_convert_fusion.4), channel_id=1, replica_groups=mesh['scen'=8,'blk'=4] {'blk'}, dimensions={1}, use_global_device_ids=true | all-gather | bytes 327680 | tf_op jit(solution)/shard_map/all_gather | solution.py:37
  148.8 21.8 %reduce-scatter.18.cloned.1.call-done = f32[64,512]{1,0:T(8,128)} async-done(((f32[64,2048]{1,0:T(8,128)}), f32[64,512]{1,0:T(8,128)}) %reduce-scatter.18.cloned.1.call-update) | async-done | bytes 131088 | tf_op jit(solution)/shard_map/reduce_scatter | solution.py:32
  171.6 5.9 %all_gather.28 = bf16[64,2048]{1,0:T(8,128)(2,1)S(1)} all-gather(bf16[64,512]{1,0:T(8,128)(2,1)S(1)} %multiply_convert_fusion.3), channel_id=1, replica_groups=mesh['scen'=8,'blk'=4] {'blk'}, dimensions={1}, use_global_device_ids=true | all-gather | bytes 327680 | tf_op jit(solution)/shard_map/all_gather | solution.py:37
  183.1 21.6 %reduce-scatter.20.cloned.1.call-done = f32[64,512]{1,0:T(8,128)} async-done(((f32[64,2048]{1,0:T(8,128)}), f32[64,512]{1,0:T(8,128)}) %reduce-scatter.20.cloned.1.call-update) | async-done | bytes 131088 | tf_op jit(solution)/shard_map/reduce_scatter | solution.py:32
  205.8 5.9 %all_gather.29 = bf16[64,2048]{1,0:T(8,128)(2,1)S(1)} all-gather(bf16[64,512]{1,0:T(8,128)(2,1)S(1)} %multiply_convert_fusion.2), channel_id=1, replica_groups=mesh['scen'=8,'blk'=4] {'blk'}, dimensions={1}, use_global_device_ids=true | all-gather | bytes 327680 | tf_op jit(solution)/shard_map/all_gather | solution.py:37
  217.1 21.8 %reduce-scatter.22.cloned.1.call-done = f32[64,512]{1,0:T(8,128)} async-done(((f32[64,2048]{1,0:T(8,128)}), f32[64,512]{1,0:T(8,128)}) %reduce-scatter.22.cloned.1.call-update) | async-done | bytes 131088 | tf_op jit(solution)/shard_map/reduce_scatter | solution.py:32
  239.9 5.9 %all_gather.30 = bf16[64,2048]{1,0:T(8,128)(2,1)S(1)} all-gather(bf16[64,512]{1,0:T(8,128)(2,1)S(1)} %multiply_convert_fusion.1), channel_id=1, replica_groups=mesh['scen'=8,'blk'=4] {'blk'}, dimensions={1}, use_global_device_ids=true | all-gather | bytes 327680 | tf_op jit(solution)/shard_map/all_gather | solution.py:37
  251.2 21.8 %reduce-scatter.24.cloned.1.call-done = f32[64,512]{1,0:T(8,128)} async-done(((f32[64,2048]{1,0:T(8,128)}), f32[64,512]{1,0:T(8,128)}) %reduce-scatter.24.cloned.1.call-update) | async-done | bytes 131088 | tf_op jit(solution)/shard_map/reduce_scatter | solution.py:32
  274.1 5.9 %all_gather.31 = bf16[64,2048]{1,0:T(8,128)(2,1)S(1)} all-gather(bf16[64,512]{1,0:T(8,128)(2,1)S(1)} %multiply_convert_fusion), channel_id=1, replica_groups=mesh['scen'=8,'blk'=4] {'blk'}, dimensions={1}, use_global_device_ids=true | all-gather | bytes 327680 | tf_op jit(solution)/shard_map/all_gather | solution.py:37
  280.0 3.1 multiply_reduce_fusion.1
  286.0 19.5 %all-reduce.1 = (f32[1024]{0:T(1024)S(1)}, f32[]{:T(128)}) all-reduce(f32[1024]{0:T(1024)S(1)} %get-tuple-element.16, f32[]{:T(128)} %reduce_sum.37), channel_id=1, replica_groups=mesh['scen'=8,'blk'=4] {'scen'}, use_global_device_ids=true, to_apply=%region_10.11 | all-reduce | flops 1025 | bytes 8200 | tf_op jit(solution)/shard_map/psum | solution.py:51
  308.7 6.3 %all-reduce.2 = (f32[]{:T(128)}, f32[]{:T(128)}) all-reduce(f32[]{:T(128)} %get-tuple-element.14, f32[]{:T(128)S(6)} %mul.128), channel_id=1, replica_groups=mesh['scen'=8,'blk'=4] {'blk'}, use_global_device_ids=true, to_apply=%region_14.15 | all-reduce | flops 2 | bytes 16 | tf_op jit(solution)/shard_map/psum | solution.py:55
  315.0 17.7 %all-reduce = (f32[]{:T(128)}, f32[]{:T(128)}) all-reduce(f32[]{:T(128)} %get-tuple-element.10, f32[]{:T(128)} %get-tuple-element.11), channel_id=1, replica_groups=mesh['scen'=8,'blk'=4] {'scen'}, use_global_device_ids=true, to_apply=%region_15.16 | all-reduce | flops 2 | bytes 16 | tf_op jit(solution)/shard_map/psum | solution.py:55
  (83 shorter events, 44.3 us)
Async XLA Ops:
  7.2 33.8 %copy-start.12 = (f32[64,1024]{1,0:T(8,128)S(1)}, f32[64,1024]{1,0:T(8,128)}, u32[]{:S(2)}) copy-start(f32[64,1024]{1,0:T(8,128)} %param.16) | copy-start | bytes 786436
  7.2 26.7 %copy-start.8 = (f32[64,2048]{1,0:T(8,128)S(1)}, f32[64,2048]{1,0:T(8,128)}, u32[]{:S(2)}) copy-start(f32[64,2048]{1,0:T(8,128)} %param.12) | copy-start | bytes 1572868
  7.2 26.7 %copy-start.9 = (f32[64,2048]{1,0:T(8,128)S(1)}, f32[64,2048]{1,0:T(8,128)}, u32[]{:S(2)}) copy-start(f32[64,2048]{1,0:T(8,128)} %param.13) | copy-start | bytes 1572868
  7.2 26.7 %copy-start.10 = (f32[64,2048]{1,0:T(8,128)S(1)}, f32[64,2048]{1,0:T(8,128)}, u32[]{:S(2)}) copy-start(f32[64,2048]{1,0:T(8,128)} %param.11) | copy-start | bytes 1572868
  7.2 33.7 %copy-start.15 = (f32[1024]{0:T(1024)S(1)}, f32[1024]{0:T(1024)}, u32[]{:S(2)}) copy-start(f32[1024]{0:T(1024)} %param.17) | copy-start | bytes 12292
  7.2 26.7 %reduce-scatter.10.cloned.1.call-start = ((), (), s32[]{:S(2)}) async-start(), calls=%async_computation.9 | async-start | bytes 655360 | tf_op jit(solution)/shard_map/reduce_scatter | solution.py:32
  11.9 56.2 %reduce-scatter.12.cloned.1.call-start = ((), (), s32[]{:S(2)}) async-start(), calls=%async_computation.10 | async-start | bytes 655360 | tf_op jit(solution)/shard_map/reduce_scatter | solution.py:32
  33.9 10.1 %copy-start = (bf16[2048,1024]{1,0:T(8,128)(2,1)S(1)}, bf16[2048,1024]{1,0:T(8,128)(2,1)}, u32[]{:S(2)}) copy-start(bf16[2048,1024]{1,0:T(8,128)(2,1)} %param.10) | copy-start | bytes 12582916
  46.3 56.0 %reduce-scatter.14.cloned.1.call-start = ((), (), s32[]{:S(2)}) async-start(), calls=%async_computation.11 | async-start | bytes 655360 | tf_op jit(solution)/shard_map/reduce_scatter | solution.py:32
  68.1 10.1 %copy-start.1 = (bf16[2048,1024]{1,0:T(8,128)(2,1)S(1)}, bf16[2048,1024]{1,0:T(8,128)(2,1)}, u32[]{:S(2)}) copy-start(bf16[2048,1024]{1,0:T(8,128)(2,1)} %param.10) | copy-start | bytes 12582916
  80.4 56.0 %reduce-scatter.16.cloned.1.call-start = ((), (), s32[]{:S(2)}) async-start(), calls=%async_computation.12 | async-start | bytes 655360 | tf_op jit(solution)/shard_map/reduce_scatter | solution.py:32
  102.2 10.1 %copy-start.2 = (bf16[2048,1024]{1,0:T(8,128)(2,1)S(1)}, bf16[2048,1024]{1,0:T(8,128)(2,1)}, u32[]{:S(2)}) copy-start(bf16[2048,1024]{1,0:T(8,128)(2,1)} %param.10) | copy-start | bytes 12582916
  114.6 56.0 %reduce-scatter.18.cloned.1.call-start = ((), (), s32[]{:S(2)}) async-start(), calls=%async_computation.13 | async-start | bytes 655360 | tf_op jit(solution)/shard_map/reduce_scatter | solution.py:32
  136.4 10.1 %copy-start.3 = (bf16[2048,1024]{1,0:T(8,128)(2,1)S(1)}, bf16[2048,1024]{1,0:T(8,128)(2,1)}, u32[]{:S(2)}) copy-start(bf16[2048,1024]{1,0:T(8,128)(2,1)} %param.10) | copy-start | bytes 12582916
  148.7 56.0 %reduce-scatter.20.cloned.1.call-start = ((), (), s32[]{:S(2)}) async-start(), calls=%async_computation.14 | async-start | bytes 655360 | tf_op jit(solution)/shard_map/reduce_scatter | solution.py:32
  170.5 10.1 %copy-start.4 = (bf16[2048,1024]{1,0:T(8,128)(2,1)S(1)}, bf16[2048,1024]{1,0:T(8,128)(2,1)}, u32[]{:S(2)}) copy-start(bf16[2048,1024]{1,0:T(8,128)(2,1)} %param.10) | copy-start | bytes 12582916
  182.9 56.0 %reduce-scatter.22.cloned.1.call-start = ((), (), s32[]{:S(2)}) async-start(), calls=%async_computation.15 | async-start | bytes 655360 | tf_op jit(solution)/shard_map/reduce_scatter | solution.py:32
  217.0 56.0 %reduce-scatter.24.cloned.1.call-start = ((), (), s32[]{:S(2)}) async-start(), calls=%async_computation.16 | async-start | bytes 655360 | tf_op jit(solution)/shard_map/reduce_scatter | solution.py:32
  238.8 10.1 %copy-start.6 = (bf16[2048,1024]{1,0:T(8,128)(2,1)S(1)}, bf16[2048,1024]{1,0:T(8,128)(2,1)}, u32[]{:S(2)}) copy-start(bf16[2048,1024]{1,0:T(8,128)(2,1)} %param.10) | copy-start | bytes 12582916
  248.9 31.1 %copy-start.18 = (f32[64]{0:T(128)S(1)}, f32[64]{0:T(128)}, u32[]{:S(2)}) copy-start(f32[64]{0:T(128)} %param.19) | copy-start | bytes 772
  251.2 83.6 %reduce-scatter.26.cloned.1.call-start = ((), (), s32[]{:S(2)}) async-start(), calls=%async_computation.17 | async-start | bytes 655360 | tf_op jit(solution)/shard_map/reduce_scatter | solution.py:46
  273.0 10.1 %copy-start.7 = (bf16[2048,1024]{1,0:T(8,128)(2,1)S(1)}, bf16[2048,1024]{1,0:T(8,128)(2,1)}, u32[]{:S(2)}) copy-start(bf16[2048,1024]{1,0:T(8,128)(2,1)} %param.10) | copy-start | bytes 12582916
  283.1 53.3 %copy-start.11 = (f32[64,1024]{1,0:T(8,128)}, f32[64,1024]{1,0:T(8,128)S(1)}, u32[]{:S(2)}) copy-start(f32[64,1024]{1,0:T(8,128)S(1)} %get-tuple-element.17) | copy-start | bytes 786436
  306.7 29.7 %copy-start.17 = (f32[1024]{0:T(1024)}, f32[1024]{0:T(1024)S(1)}, u32[]{:S(2)}) copy-start(f32[1024]{0:T(1024)S(1)} %get-tuple-element.13) | copy-start | bytes 12292
  (4 other events, 24.5 us)
Sparse Core Ops, SparseCore 0:
  12.0 21.8 reduce-scatter.9
  46.4 21.6 reduce-scatter.11
  80.5 21.6 reduce-scatter.13
  114.7 21.6 reduce-scatter.15
  148.8 21.6 reduce-scatter.17
  183.0 21.6 reduce-scatter.19
  217.1 21.6 reduce-scatter.21
  251.3 21.6 reduce-scatter.23
  285.5 21.6 reduce-scatter.25
